TPU v7x, 32 devices: a whole 2x2x4 slice. The times are simulated.
32 devices in a mesh: fsdp: 4 (over y, x), tenant: 4 (over z), dp: 2 (over core).
Axes of the slice: x: 2, y: 2, z: 4, core: 2. Of those that a mesh axis runs over, the one named last changes fastest.
Arguments:
- tokens: bfloat16 [3072, 5120], P(('fsdp', 'dp'), 'tenant'), may hold values from -6 to 6
- block_tenant_index: int32 [48], P(('fsdp', 'dp')), may hold values from 0 to 7
- ranks: int32 [8], replicated, may hold values from 16 to 64, as said below
- frozen_up_weight: bfloat16 [5120, 14336], P(('fsdp', 'dp'), 'tenant'), may hold values from -0.078125 to 0.078125
- tenant_down_adapters: bfloat16 [8, 64, 5120], P('tenant'), may hold values from -0.078125 to 0.078125
- tenant_up_adapters: bfloat16 [8, 64, 14336], P('tenant'), may hold values from -0.75 to 0.75
- cotangent: bfloat16 [3072, 14336], P(('fsdp', 'dp'), 'tenant'), may hold values from -6 to 6
Outputs:
- hidden_out: bfloat16 [3072, 14336], P(('fsdp', 'dp'), 'tenant')
- grad_tokens: bfloat16 [3072, 5120], P(('fsdp', 'dp'), 'tenant')
- grad_down: float32 [8, 64, 5120], P('dp', None, 'tenant')
- grad_up: float32 [8, 64, 14336], P('dp', None, 'tenant')
Inputs may be any that keep to these rules, and one draw needn't show every extreme that they name: `ranks`: multiples of 16; some tenant has rank 64.
All inputs are finite; a program needn't handle non-finite values.
Results may differ from a plain program's by a relative error of at most 0.0034.
Values may be sent and summed in bfloat16 or wider, within the bound.
A program may use at most 128 MiB of HBM per device.

v0:
```python
import jax
import jax.numpy as jnp
from jax import lax
from jax.sharding import PartitionSpec as P

BLOCK = 64


alpha_scale = 32.0


def make_gain(block_tenant_index, ranks, rows, largest_rank):
    tenants = ranks.shape[0]
    rows_tenant = jnp.repeat(block_tenant_index, BLOCK, total_repeat_length=rows)
    columns = jnp.arange(tenants * largest_rank, dtype=jnp.int32)
    col_tenant = columns // largest_rank
    col_slot = columns % largest_rank
    ranks_col = jnp.repeat(ranks, largest_rank, total_repeat_length=tenants * largest_rank)
    keep = (rows_tenant[:, None] == col_tenant[None, :]) & (col_slot[None, :] < ranks_col[None, :])
    scale_col = alpha_scale / ranks_col.astype(jnp.float32)
    return jnp.where(keep, scale_col[None, :], jnp.float32(0.0))


def shards(
    tokens,
    block_tenant_index,
    ranks,
    frozen_up_weight,
    tenant_down_adapters,
    tenant_up_adapters,
    cotangent,
):
    rows = tokens.shape[0]
    local_d = tokens.shape[1]
    local_f = cotangent.shape[1]
    tenants = ranks.shape[0]
    largest_rank = tenant_down_adapters.shape[1]
    gain = make_gain(block_tenant_index, ranks, rows, largest_rank)
    whole = lax.all_gather(tokens, "tenant", axis=1, tiled=True)
    weight = lax.all_gather(frozen_up_weight, ("fsdp", "dp"), axis=0, tiled=True)
    down_part, up_adapter_slice = (
        lax.all_to_all(tenant_down_adapters, "tenant", split_axis=2, concat_axis=0, tiled=True),
        lax.all_to_all(tenant_up_adapters, "tenant", split_axis=2, concat_axis=0, tiled=True),
    )
    local_down = down_part.reshape(tenants * largest_rank, local_d)
    partial_proj = lax.dot_general(
        tokens, local_down, (((1,), (1,)), ((), ())), preferred_element_type=jnp.float32
    )
    proj = lax.psum(partial_proj, "tenant")
    flattened_up = up_adapter_slice.reshape(tenants * largest_rank, local_f)
    adapted = (proj * gain).astype(jnp.bfloat16)
    base = jnp.dot(whole, weight, preferred_element_type=jnp.float32)
    hidden_out = (base + jnp.dot(adapted, flattened_up, preferred_element_type=jnp.float32)).astype(
        jnp.bfloat16
    )
    back_part = lax.dot_general(
        cotangent, flattened_up, (((1,), (1,)), ((), ())), preferred_element_type=jnp.float32
    )
    back = lax.psum(back_part, "tenant")
    adapted_grad = (back * gain).astype(jnp.bfloat16)
    base_back = lax.dot_general(
        cotangent, weight, (((1,), (1,)), ((), ())), preferred_element_type=jnp.float32
    )
    grad_base = lax.psum_scatter(base_back, "tenant", scatter_dimension=1, tiled=True)
    grad_tokens = (
        grad_base + jnp.dot(adapted_grad, local_down, preferred_element_type=jnp.float32)
    ).astype(jnp.bfloat16)
    up_term = lax.dot_general(
        adapted, cotangent, (((0,), (0,)), ((), ())), preferred_element_type=jnp.float32
    )
    down_term = lax.dot_general(
        adapted_grad, tokens, (((0,), (0,)), ((), ())), preferred_element_type=jnp.float32
    )
    up_term = up_term.reshape(tenants, largest_rank, local_f)
    down_term = down_term.reshape(tenants, largest_rank, local_d)
    down_share, up_share = (
        lax.psum_scatter(down_term, "dp", scatter_dimension=0, tiled=True),
        lax.psum_scatter(up_term, "dp", scatter_dimension=0, tiled=True),
    )
    grad_down, grad_up = lax.psum((down_share, up_share), "fsdp")
    return (hidden_out, grad_tokens, grad_down, grad_up)


def solution(mesh):
    return jax.shard_map(
        shards,
        mesh=mesh,
        in_specs=(
            P(("fsdp", "dp"), "tenant"),
            P(("fsdp", "dp")),
            P(),
            P(("fsdp", "dp"), "tenant"),
            P("tenant", None, None),
            P("tenant", None, None),
            P(("fsdp", "dp"), "tenant"),
        ),
        out_specs=(
            P(("fsdp", "dp"), "tenant"),
            P(("fsdp", "dp"), "tenant"),
            P("dp", None, "tenant"),
            P("dp", None, "tenant"),
        ),
        check_vma=False,
    )
```

profile of v0, /device:TPU:0, one launch (start us, length us, event | category | flops | bytes accessed | tf_op | source)
XLA Modules:
  0.0 692.7 jit_solution(15375952981959615952)
XLA Ops:
  8.0 0.0 copy-start
  8.0 6.4 copy.13
  14.5 4.7 reshape.322
  19.1 6.3 all-to-all-start
  25.5 15.8 %copy.16 = bf16[2,64,14336]{1,0,2:T(2,128)(2,1)} copy(bf16[2,64,14336]{2,1,0:T(8,128)(2,1)} %param.16) | data formatting | bytes 7340032 | tf_op args[5]
  41.3 8.6 %reshape.320 = bf16[4,2,229376]{2,1,0:T(2,128)(2,1)} reshape(bf16[14336,2,64]{2,1,0:T(2,128)(2,1)} %bitcast.77) | data formatting | bytes 7340032
  49.9 7.1 %all-to-all-done = bf16[4,2,81920]{2,1,0:T(2,128)(2,1)} async-done(((bf16[4,2,81920]{2,1,0:T(2,128)(2,1)}), bf16[4,2,81920]{2,1,0:T(2,128)(2,1)}, u32[]{:S(2)}, u32[]{:S(2)}) %all-to-all-start) | async-done | bytes 1310752 | tf_op jit(solution)/shard_map/all_to_all | solution.py:42
  56.9 4.8 all-to-all-start.1
  61.8 0.0 all-reduce.5.cloned.1.call-start
  61.8 4.6 reshape.323
  66.4 7.4 %copy.19 = bf16[2,64,4,1280]{3,2,1,0:T(4,128)(2,1)} copy(bf16[2,64,4,1280]{1,0,3,2:T(2,128)(2,1)} %bitcast.82) | data formatting | bytes 2621440 | tf_op jit(solution)/shard_map/all_to_all | solution.py:42
  73.8 1.4 copy.15
  75.3 0.0 copy-start.3
  75.3 1.0 copy-done.3
  76.3 2.8 fusion.26
  79.1 64.2 %all-to-all-done.1 = bf16[4,2,229376]{2,1,0:T(2,128)(2,1)} async-done(((bf16[4,2,229376]{2,1,0:T(2,128)(2,1)}), bf16[4,2,229376]{2,1,0:T(2,128)(2,1)}, u32[]{:S(2)}, u32[]{:S(2)}) %all-to-all-start.1) | async-done | bytes 3670048 | tf_op jit(solution)/shard_map/all_to_all | solution.py:43
  143.3 8.4 %reshape.321 = bf16[14336,2,64]{2,1,0:T(2,128)(2,1)} reshape(bf16[4,2,229376]{2,1,0:T(2,128)(2,1)} %all-to-all-done.1) | data formatting | bytes 7340032
  151.7 18.7 %copy.20 = bf16[2,64,4,3584]{3,2,1,0:T(4,128)(2,1)} copy(bf16[2,64,4,3584]{1,0,3,2:T(2,128)(2,1)} %bitcast.76) | data formatting | bytes 7340032 | tf_op jit(solution)/shard_map/all_to_all | solution.py:43
  170.4 2.7 copy.18
  173.1 0.0 copy-start.2
  173.1 1.8 copy-done.2
  174.9 0.0 copy-done
  174.9 2.5 fusion.28
  177.4 0.0 all-reduce.5.cloned.1.call-update
  177.5 0.0 all-gather.5.cloned.1.call-start
  177.5 0.5 all-gather.5.cloned.1.call-update
  178.0 0.0 reduce-scatter.6.cloned.1.call-start
  178.1 0.0 copy-done.8
  178.1 0.7 fusion.23
  178.8 0.0 copy-done.7
  178.8 0.7 fusion.24
  179.5 0.0 copy-done.10
  179.5 0.1 add_add_fusion.1
  179.6 0.1 fusion.8
  179.7 3.8 fusion.16
  183.5 4.5 compare_select_fusion.2
  188.0 0.8 fusion.12
  188.8 0.1 and_select_fusion
  188.9 56.8 %all-reduce.5.cloned.1.call-done = (f32[384,512]{1,0:T(8,128)}, f32[384,512]{1,0:T(8,128)}) async-done(((f32[384,512]{1,0:T(8,128)}, f32[384,512]{1,0:T(8,128)}), (f32[384,512]{1,0:T(8,128)}, f32[384,512]{1,0:T(8,128)})) %all-reduce.5.cloned.1.call-update) | async-done | bytes 1572880 | tf_op jit(solution)/shard_map/psum | solution.py:49
  245.7 4.0 fusion.17
  249.7 0.0 reduce-scatter.6.cloned.1.call-update
  249.7 0.0 reduce-scatter.8.cloned.1.call-start
  249.8 0.0 copy-done.5
  249.8 7.1 %fusion.20 = f32[512,3584]{1,0:T(8,128)} fusion(bf16[384,3584]{1,0:T(8,128)(2,1)S(1)} %copy-done, f32[384,512]{1,0:T(8,128)S(1)} %copy-done.5, f32[512]{0:T(512)S(1)} %convert_divide_fusion, s32[512]{0:T(512)S(1)} %add_select_fusion, s32[384]{0:T(512)S(1)} %and_select_fusion, pred[512]{0:T(512)(128)(4,1)S(1)} %get-tuple-element.32), kind=kOutput, calls=%fused_computation.52 | convolution fusion | flops 1410269184 | bytes 10885120 | tf_op jit(solution)/shard_map/dot_general | solution.py:68
  256.9 0.0 reduce-scatter.8.cloned.1.call-update
  256.9 0.0 all-gather.3.cloned.1.call-start
  256.9 0.5 all-gather.3.cloned.1.call-update
  257.5 0.2 reduce-scatter.4.cloned.1.call-start
  257.7 96.2 %all-gather.5.cloned.1.call-done = bf16[5120,3584]{1,0:T(8,128)(2,1)} async-done(((bf16[640,3584]{1,0:T(8,128)(2,1)}), bf16[5120,3584]{1,0:T(8,128)(2,1)}) %all-gather.5.cloned.1.call-update) | async-done | bytes 36700176 | tf_op jit(solution)/shard_map/all_gather | solution.py:40
  353.9 22.1 %fusion.27 = f32[384,5120]{1,0:T(8,128)} fusion(bf16[384,3584]{1,0:T(8,128)(2,1)S(1)} %copy-done, bf16[5120,3584]{1,0:T(8,128)(2,1)} %all-gather.5.cloned.1.call-done), kind=kOutput, calls=%fused_computation.57 | convolution fusion | flops 14092861440 | bytes 47316992 | tf_op jit(solution)/shard_map/dot_general | solution.py:61
  376.0 0.0 reduce-scatter.4.cloned.1.call-update
  376.0 0.0 all-reduce.7.cloned.1.call-start
  376.1 0.0 reduce-scatter.6.cloned.1.call-done
  376.1 0.0 reduce-scatter.8.cloned.1.call-done
  376.1 0.5 all-reduce.7.cloned.1.call-update
  376.6 139.9 %all-gather.3.cloned.1.call-done = bf16[384,5120]{1,0:T(8,128)(2,1)} async-done(((bf16[384,1280]{1,0:T(8,128)(2,1)}), bf16[384,5120]{1,0:T(8,128)(2,1)}) %all-gather.3.cloned.1.call-update) | async-done | bytes 3932176 | tf_op jit(solution)/shard_map/all_gather | solution.py:39
  516.5 23.5 %fusion.25 = f32[384,3584]{1,0:T(8,128)} fusion(bf16[384,5120]{1,0:T(8,128)(2,1)} %all-gather.3.cloned.1.call-done, bf16[5120,3584]{1,0:T(8,128)(2,1)} %all-gather.5.cloned.1.call-done), kind=kOutput, calls=%fused_computation.55 | convolution fusion | flops 14092861440 | bytes 46137344 | tf_op jit(solution)/shard_map/dot_general | solution.py:52
  540.0 7.0 %fusion = bf16[384,3584]{1,0:T(8,128)(2,1)} fusion(f32[384,3584]{1,0:T(8,128)} %fusion.25, bf16[512,3584]{1,0:T(8,128)(2,1)} %bitcast.79, f32[384,512]{1,0:T(8,128)S(1)} %copy-done.5, f32[512]{0:T(512)S(1)} %convert_divide_fusion, s32[512]{0:T(512)S(1)} %add_select_fusion, s32[384]{0:T(512)S(1)} %and_select_fusion, pred[512]{0:T(512)(128)(4,1)S(1)} %get-tuple-element.32), kind=kOutput, calls=%fused_computation.1 | convolution fusion | flops 1413021696 | bytes 12720128 | tf_op jit(solution)/shard_map/dot_general | solution.py:53
  547.0 10.7 %reduce-scatter.4.cloned.1.call-done = f32[384,1280]{1,0:T(8,128)} async-done(((f32[384,5120]{1,0:T(8,128)}), f32[384,1280]{1,0:T(8,128)}) %reduce-scatter.4.cloned.1.call-update) | async-done | bytes 1966096 | tf_op jit(solution)/shard_map/reduce_scatter | solution.py:64
  557.7 0.0 copy-done.4
  557.7 3.3 fusion.1
  561.0 117.8 %all-reduce.7.cloned.1.call-done = (f32[4,64,1280]{2,1,0:T(8,128)}, f32[4,64,3584]{2,1,0:T(8,128)}) async-done(((f32[4,64,1280]{2,1,0:T(8,128)}, f32[4,64,3584]{2,1,0:T(8,128)}), (f32[4,64,1280]{2,1,0:T(8,128)}, f32[4,64,3584]{2,1,0:T(8,128)})) %all-reduce.7.cloned.1.call-update) | async-done | bytes 4980752 | tf_op jit(solution)/shard_map/psum | solution.py:80
  678.8 2.6 copy.29
  681.4 4.1 copy.30
  (16 shorter events, 0.1 us)
Async XLA Ops:
  8.0 166.9 %copy-start = (bf16[384,3584]{1,0:T(8,128)(2,1)S(1)}, bf16[384,3584]{1,0:T(8,128)(2,1)}, u32[]{:S(2)}) copy-start(bf16[384,3584]{1,0:T(8,128)(2,1)} %param.17) | copy-start | bytes 8257540
  19.1 37.8 %all-to-all-start = ((bf16[4,2,81920]{2,1,0:T(2,128)(2,1)}), bf16[4,2,81920]{2,1,0:T(2,128)(2,1)}, u32[]{:S(2)}, u32[]{:S(2)}) async-start(bf16[4,2,81920]{2,1,0:T(2,128)(2,1)} %reshape.322), calls=%async_computation | async-start | bytes 2621440 | tf_op jit(solution)/shard_map/all_to_all | solution.py:42
  56.9 86.3 %all-to-all-start.1 = ((bf16[4,2,229376]{2,1,0:T(2,128)(2,1)}), bf16[4,2,229376]{2,1,0:T(2,128)(2,1)}, u32[]{:S(2)}, u32[]{:S(2)}) async-start(bf16[4,2,229376]{2,1,0:T(2,128)(2,1)} %reshape.320), calls=%async_computation.1 | async-start | bytes 7340032 | tf_op jit(solution)/shard_map/all_to_all | solution.py:43
  61.8 184.0 %all-reduce.5.cloned.1.call-start = ((), (), s32[]{:S(2)}) async-start(), calls=%async_computation.10 | async-start | bytes 3145728 | tf_op jit(solution)/shard_map/psum | solution.py:49
  75.3 1.1 copy-start.3
  173.1 1.8 copy-start.2
  177.4 0.7 copy-start.8
  177.4 1.4 copy-start.7
  177.4 2.1 copy-start.10
  177.4 2.2 copy-start.9
  177.5 176.5 %all-gather.5.cloned.1.call-start = ((), (), s32[]{:S(2)}) async-start(), calls=%async_computation.6 | async-start | bytes 41287680 | tf_op jit(solution)/shard_map/all_gather | solution.py:40
  178.0 198.0 %reduce-scatter.6.cloned.1.call-start = ((), (), s32[]{:S(2)}) async-start(), calls=%async_computation.8 | async-start | bytes 3932160 | tf_op jit(solution)/shard_map/reduce_scatter | solution.py:77
  245.7 4.1 copy-start.5
  249.7 126.4 %reduce-scatter.8.cloned.1.call-start = ((), (), s32[]{:S(2)}) async-start(), calls=%async_computation.9 | async-start | bytes 11010048 | tf_op jit(solution)/shard_map/reduce_scatter | solution.py:78
  256.9 259.6 %all-gather.3.cloned.1.call-start = ((), (), s32[]{:S(2)}) async-start(), calls=%async_computation.5 | async-start | bytes 4915200 | tf_op jit(solution)/shard_map/all_gather | solution.py:39
  257.5 300.2 %reduce-scatter.4.cloned.1.call-start = ((), (), s32[]{:S(2)}) async-start(), calls=%async_computation.7 | async-start | bytes 9830400 | tf_op jit(solution)/shard_map/reduce_scatter | solution.py:64
  376.0 302.8 %all-reduce.7.cloned.1.call-start = ((), (), s32[]{:S(2)}) async-start(), calls=%async_computation.11 | async-start | bytes 9961472 | tf_op jit(solution)/shard_map/psum | solution.py:80
  540.0 17.8 %copy-start.4 = (bf16[4,2,64,1280]{3,2,1,0:T(8,128)(2,1)S(1)}, bf16[4,2,64,1280]{3,2,1,0:T(8,128)(2,1)}, u32[]{:S(2)}) copy-start(bf16[4,2,64,1280]{3,2,1,0:T(8,128)(2,1)} %copy-done.3) | copy-start | bytes 3932164
  540.0 17.8 %copy-start.6 = (f32[384,512]{1,0:T(8,128)S(1)}, f32[384,512]{1,0:T(8,128)}, u32[]{:S(2)}) copy-start(f32[384,512]{1,0:T(8,128)} %get-tuple-element.29) | copy-start | bytes 2359300
  678.8 6.8 copy-start.1
Sparse Core Ops, SparseCore 0:
  177.6 68.0 all-reduce.4
  249.9 16.8 reduce-scatter.5
  269.1 17.2 reduce-scatter.7
  376.1 181.5 reduce-scatter.3
  561.2 117.5 all-reduce.6
Sparse Core Ops, SparseCore 1:
  179.9 174.0 all-gather.4
  355.4 161.1 all-gather.2
where the time goes:
time: 695 us; the launch traced here: 693 us
  waiting for transfers between devices  494 us (71%)
  local copies, waits for them, and re-layouts  89.8 us (13%)
  matrix products  72.2 us (10%)
  between operations  15.4 us (2%)
  starting transfers between devices  11.6 us (2%)
  other arithmetic  9.35 us (1%)
    all_gather x1, waiting for transfers between devices, shards(): whole = lax.all_gather(tokens, 'tenant', axis=1, tiled=True)  140 us
    psum x1, waiting for transfers between devices, shards(): grad_down, grad_up = lax.psum((down_share, up_share), 'fsdp')  118 us
    all_gather x1, waiting for transfers between devices, shards(): lax.all_gather(frozen_up_weight, ('fsdp', 'dp'), axis=0, tiled=True)  96.2 us
    all_to_all x1, waiting for transfers between devices, shards(): lax.all_to_all(tenant_up_adapters, 'tenant', split_axis=2, concat_axis=0,...  64.2 us
    unnamed x30, local copies, waits for them, and re-layouts  58.2 us
    psum x1, waiting for transfers between devices, shards(): proj = lax.psum(partial_proj, 'tenant')  56.8 us
    dot_general x1, matrix products, shards(): base = jnp.dot(whole, weight, preferred_element_type=jnp.float32)  23.5 us
    dot_general x1, matrix products, shards(): lax.dot_general(cotangent, weight, (((1,), (1,)), ((), ())), preferred_el...  22.1 us
  transfers between devices with their start and end apart: 9, of which 7 were waited for; matrix products, arithmetic and copies ran while one was open for 17% of the time, Pallas kernels for 0%

commit v1 on v0

v1 whole, which is shorter than its diff:
```python
import jax
import jax.numpy as jnp
from jax import lax
from jax.sharding import PartitionSpec as P

BLOCK = 64


alpha_scale = 32.0

BF16 = jnp.bfloat16
F32 = jnp.float32


def nt(a, b):
    return lax.dot_general(a, b, (((1,), (1,)), ((), ())), preferred_element_type=F32)


def tn(a, b):
    return lax.dot_general(a, b, (((0,), (0,)), ((), ())), preferred_element_type=F32)


def fetch_adapter(adapter, tenant_n, dp_n):
    share = adapter.shape[1] // dp_n
    mine = lax.dynamic_slice_in_dim(adapter, lax.axis_index("dp") * share, share, axis=1)
    part = lax.all_to_all(mine, "tenant", split_axis=2, concat_axis=0, tiled=True)
    return lax.all_gather(part, "dp", axis=1, tiled=True)


def reduce_fsdp(x, fsdp_n):
    rows = x.shape[0]
    got = lax.all_to_all(
        x.astype(BF16).reshape(fsdp_n, rows // fsdp_n, x.shape[1]), "fsdp", 0, 0, tiled=True
    )
    total = jnp.sum(got.astype(F32), axis=0).astype(BF16)
    return lax.all_gather(total, "fsdp", axis=0, tiled=True).astype(F32)


def make_shards(mesh):
    tenant_n, fsdp_n, dp_n = mesh.shape["tenant"], mesh.shape["fsdp"], mesh.shape["dp"]

    def shards(tokens, block_tenant_index, ranks, frozen_up_weight, tenant_down_adapters,
               tenant_up_adapters, cotangent):
        rows, local_d = tokens.shape
        local_f = cotangent.shape[1]
        tenants = ranks.shape[0]
        rank = tenant_down_adapters.shape[1]
        depth = frozen_up_weight.shape[0]
        blocks = fsdp_n * dp_n

        first = max(128, (depth * 3 // 5) // 128 * 128) if depth > 128 else depth
        cuts = [(0, first)] + ([(first, depth)] if first < depth else [])
        weights = [
            lax.all_gather(frozen_up_weight[a:b], ("fsdp", "dp"), axis=0, tiled=True)
            for a, b in cuts
        ]
        up = fetch_adapter(tenant_up_adapters, tenant_n, dp_n).reshape(tenants * rank, local_f)
        down = fetch_adapter(tenant_down_adapters, tenant_n, dp_n).reshape(tenants * rank, local_d)

        onehot = (block_tenant_index[:, None] == jnp.arange(tenants, dtype=jnp.int32)[None, :])
        sel = onehot.astype(F32)[:, None, :, None]
        own_rank = jnp.sum(jnp.where(onehot, ranks[None, :], 0), axis=1)
        keep = jnp.arange(rank, dtype=jnp.int32)[None, :] < own_rank[:, None]
        gain = jnp.where(keep, (alpha_scale / own_rank.astype(F32))[:, None], F32(0.0))

        def compact(full):
            full = full.reshape(rows // BLOCK, BLOCK, tenants, rank)
            return jnp.sum(full * sel, axis=2)

        both = jnp.concatenate([compact(nt(tokens, down)), compact(nt(cotangent, up))], axis=2)
        both = lax.psum(both, "tenant")

        def spread(values):
            scaled = (values * gain[:, None, :]).astype(BF16)
            return (scaled[:, :, None, :] * sel.astype(BF16)).reshape(rows, tenants * rank)

        adapted = spread(both[:, :, :rank])
        adapted_grad = spread(both[:, :, rank:])

        terms = jnp.concatenate([tn(adapted, cotangent), tn(adapted_grad, tokens)], axis=1)
        terms = lax.psum_scatter(terms, "dp", scatter_dimension=0, tiled=True)
        grads = reduce_fsdp(terms, fsdp_n)
        grad_up = grads[:, :local_f].reshape(tenants // dp_n, rank, local_f)
        grad_down = grads[:, local_f:].reshape(tenants // dp_n, rank, local_d)

        whole = lax.all_gather(tokens, "tenant", axis=1, tiled=True)
        whole3 = whole.reshape(rows, blocks, depth)
        hidden = jnp.dot(adapted, up, preferred_element_type=F32)
        pieces = []
        for (a, b), weight in zip(cuts, weights):
            back = nt(cotangent, weight).astype(BF16)
            n = b - a
            got = lax.all_to_all(
                back.reshape(rows, tenant_n, blocks * n // tenant_n).transpose(1, 0, 2),
                "tenant", 0, 0, tiled=True,
            )
            pieces.append(jnp.sum(got.astype(F32), axis=0).reshape(rows, blocks // tenant_n, n))
            hidden = hidden + jnp.dot(
                whole3[:, :, a:b].reshape(rows, blocks * n), weight, preferred_element_type=F32
            )
        hidden_out = hidden.astype(BF16)
        grad_base = jnp.concatenate(pieces, axis=2).reshape(rows, local_d)
        grad_tokens = (
            grad_base + jnp.dot(adapted_grad, down, preferred_element_type=F32)
        ).astype(BF16)
        return (hidden_out, grad_tokens, grad_down, grad_up)

    return shards


def solution(mesh):
    return jax.shard_map(
        make_shards(mesh),
        mesh=mesh,
        in_specs=(
            P(("fsdp", "dp"), "tenant"),
            P(("fsdp", "dp")),
            P(),
            P(("fsdp", "dp"), "tenant"),
            P("tenant", None, None),
            P("tenant", None, None),
            P(("fsdp", "dp"), "tenant"),
        ),
        out_specs=(
            P(("fsdp", "dp"), "tenant"),
            P(("fsdp", "dp"), "tenant"),
            P("dp", None, "tenant"),
            P("dp", None, "tenant"),
        ),
        check_vma=False,
    )
```

time: 695 us -> 598 us (0.86)
  waiting for transfers between devices: 494 us -> 338 us
  local copies, waits for them, and re-layouts: 89.8 us -> 111 us
  other arithmetic: 9.35 us -> 27.8 us
  starting transfers between devices: 11.6 us -> 25.8 us
    psum x2 -> x1, waiting for transfers between devices: 175 us -> 35.2 us  [shards(): both = lax.psum(both, 'tenant')]
    all_gather x1 -> x5, waiting for transfers between devices: 96.2 us -> 198 us  [the longest x2 188 us: shards(): lax.all_gather(frozen_up_weight[a:b], ('fsdp', 'dp'), axis=0, tiled=True)]
    all_gather x1, waiting for transfers between devices: 140 us -> 48 us  [shards(): whole = lax.all_gather(tokens, 'tenant', axis=1, tiled=True)]
    all_to_all x2 -> x5, waiting for transfers between devices: 71.2 us -> 44.5 us  [the longest x2 32.3 us: fetch_adapter(): lax.all_to_all(mine, 'tenant', split_axis=2, concat_axis=0, tiled=True)]
    all_to_all x2 -> x5, starting transfers between devices: 11.2 us -> 25.3 us  [the longest x2 11.4 us: fetch_adapter(): lax.all_to_all(mine, 'tenant', split_axis=2, concat_axis=0, tiled=True)]
    slice x0 -> x6, local copies, waits for them, and re-layouts: none -> 11.4 us  [the longest x2 6.44 us: shards(): frozen_up_weight[a:b]]
    concatenate x0 -> x3, other arithmetic: none -> 11.1 us  [the longest x1 8.28 us: shards(): jnp.concatenate([tn(adapted, cotangent), tn(adapted_grad, tokens)], axis=1)]
    reduce_sum x0 -> x5, other arithmetic: none -> 10 us  [the longest x2 3.83 us: shards(): jnp.sum(got.astype(F32), axis=0).reshape(rows, blocks // tenant_n, n)]
  transfers between devices with their start and end apart: 9 -> 13, of which waited for: 7 -> 9; matrix products, arithmetic and copies ran while one was open for 17% -> 32% of each run, Pallas kernels for 0% -> 0%
where the time goes in v1:
time: 598 us; the launch traced here: 596 us
  waiting for transfers between devices  338 us (57%)
  local copies, waits for them, and re-layouts  111 us (19%)
  matrix products  79 us (13%)
  other arithmetic  27.8 us (5%)
  starting transfers between devices  25.8 us (4%)
  between operations  14.3 us (2%)
    all_gather x2, waiting for transfers between devices, shards(): lax.all_gather(frozen_up_weight[a:b], ('fsdp', 'dp'), axis=0, tiled=True)  188 us
    unnamed x26, local copies, waits for them, and re-layouts  51 us
    all_gather x1, waiting for transfers between devices, shards(): whole = lax.all_gather(tokens, 'tenant', axis=1, tiled=True)  48 us
    psum x1, waiting for transfers between devices, shards(): both = lax.psum(both, 'tenant')  35.2 us
    all_to_all x2, waiting for transfers between devices, fetch_adapter(): lax.all_to_all(mine, 'tenant', split_axis=2, concat_axis=0, tiled=True)  32.3 us
    dot_general x4, matrix products, nt(): lax.dot_general(a, b, (((1,), (1,)), ((), ())), preferred_element_type=F32)  31.8 us
    dot_general x2, matrix products, shards(): jnp.dot(whole3[:, :, a:b].reshape(rows, blocks * n), weight, preferred_el...  30.3 us
    all_to_all x4, local copies, waits for them, and re-layouts, fetch_adapter(): lax.all_to_all(mine, 'tenant', split_axis=2, concat_axis=0, tiled=True)  28.3 us
  transfers between devices with their start and end apart: 13, of which 9 were waited for; matrix products, arithmetic and copies ran while one was open for 32% of the time, Pallas kernels for 0%

profile of v1, /device:TPU:0, one launch (start us, length us, event | category | flops | bytes accessed | tf_op | source)
XLA Modules:
  0.0 595.5 jit_solution(8852192433115120866)
XLA Ops:
  7.2 1.3 constant_dynamic-slice_fusion.1
  8.5 4.0 copy.30
  12.5 4.9 reshape.171
  17.4 6.3 %all-to-all-start = ((bf16[4,2,40960]{2,1,0:T(2,128)(2,1)}), bf16[4,2,40960]{2,1,0:T(2,128)(2,1)S(1)}, u32[]{:S(2)}, u32[]{:S(2)}) async-start(bf16[4,2,40960]{2,1,0:T(2,128)(2,1)} %reshape.171), calls=%async_computation | async-start | bytes 1310720 | tf_op jit(solution)/shard_map/all_to_all | solution.py:26
  23.8 2.8 constant_dynamic-slice_fusion
  26.6 15.2 %copy.31 = bf16[2,32,14336]{1,0,2:T(2,128)(2,1)} copy(bf16[2,32,14336]{2,1,0:T(8,128)(2,1)} %constant_dynamic-slice_fusion) | data formatting | bytes 3670016
  41.9 9.4 %reshape.173 = bf16[4,2,114688]{2,1,0:T(2,128)(2,1)} reshape(bf16[14336,2,32]{2,1,0:T(2,128)(2,1)} %bitcast.65) | data formatting | bytes 3670016
  51.3 5.1 all-to-all-start.1
  56.4 2.6 reshape.172
  59.0 6.2 %copy.28 = bf16[2,32,4,1280]{3,2,1,0:T(4,128)(2,1)S(1)} copy(bf16[2,32,4,1280]{1,0,3,2:T(2,128)(2,1)} %bitcast.70) | data formatting | bytes 1310720 | tf_op jit(solution)/shard_map/all_to_all | solution.py:26
  65.2 0.9 copy.20
  66.2 32.3 %all-to-all-done.1 = bf16[4,2,114688]{2,1,0:T(2,128)(2,1)} async-done(((bf16[4,2,114688]{2,1,0:T(2,128)(2,1)}), bf16[4,2,114688]{2,1,0:T(2,128)(2,1)}, u32[]{:S(2)}, u32[]{:S(2)}) %all-to-all-start.1) | async-done | bytes 1835040 | tf_op jit(solution)/shard_map/all_to_all | solution.py:26
  98.5 6.9 %reshape.174 = bf16[14336,2,32]{2,1,0:T(2,128)(2,1)} reshape(bf16[4,2,114688]{2,1,0:T(2,128)(2,1)} %all-to-all-done.1) | data formatting | bytes 3670016
  105.4 18.1 %copy.29 = bf16[2,32,4,3584]{3,2,1,0:T(4,128)(2,1)} copy(bf16[2,32,4,3584]{1,0,3,2:T(2,128)(2,1)} %bitcast.66) | data formatting | bytes 3670016 | tf_op jit(solution)/shard_map/all_to_all | solution.py:26
  123.5 3.0 copy.24
  126.7 3.3 convolution_bitcast_fusion.1
  130.1 1.4 copy.21
  131.5 1.5 reshape.157
  132.9 5.8 all-gather.9.cloned.1.call-done
  138.7 5.0 convolution_bitcast_fusion
  143.7 1.4 copy.25
  145.1 1.5 reshape.159
  146.6 2.9 multiply_reduce_fusion.1
  149.5 0.8 pad_maximum_fusion.2
  151.4 35.2 %all-reduce.2.cloned.1.call-done = f32[6,64,128]{2,1,0:T(8,128)} async-done(((f32[6,64,128]{2,1,0:T(8,128)}), f32[6,64,128]{2,1,0:T(8,128)}) %all-reduce.2.cloned.1.call-update) | async-done | bytes 196624 | tf_op jit(solution)/shard_map/psum | solution.py:71
  186.7 1.1 fusion.3
  187.8 1.4 broadcast_multiply_fusion
  189.2 1.7 mul.91
  190.9 1.8 mul.87
  192.7 3.6 fusion.11
  196.3 5.0 fusion.10
  201.3 8.3 %pad_maximum_fusion = f32[512,4864]{1,0:T(8,128)} fusion(f32[512,1280]{1,0:T(8,128)} %fusion.11, f32[512,3584]{1,0:T(8,128)} %fusion.10), kind=kLoop, calls=%fused_computation | loop fusion | flops 2490368 | bytes 19922944 | tf_op jit(solution)/shard_map/concatenate | solution.py:80
  209.7 2.9 slice.28
  212.6 3.5 slice.26
  216.2 48.0 %all-gather.11.cloned.1.call-done = bf16[384,5120]{1,0:T(8,128)(2,1)} async-done(((bf16[384,1280]{1,0:T(8,128)(2,1)}), bf16[384,5120]{1,0:T(8,128)(2,1)}) %all-gather.11.cloned.1.call-update) | async-done | bytes 3932176 | tf_op jit(solution)/shard_map/all_gather | solution.py:86
  264.2 2.9 copy.34
  267.5 1.9 copy.35
  269.5 1.7 copy.36
  271.1 11.4 %reduce-scatter.2.cloned.1.call-done = f32[256,4864]{1,0:T(8,128)} async-done(((f32[512,4864]{1,0:T(8,128)}), f32[256,4864]{1,0:T(8,128)}) %reduce-scatter.2.cloned.1.call-update) | async-done | bytes 4980752 | tf_op jit(solution)/shard_map/reduce_scatter | solution.py:81
  282.5 4.1 convert_element_type.69
  286.6 4.6 all-to-all-start.4
  291.2 6.6 %fusion.8 = f32[384,3584]{1,0:T(8,128)} fusion(bf16[384,512]{1,0:T(8,128)(2,1)S(1)} %mul.87, bf16[512,3584]{1,0:T(8,128)(2,1)} %bitcast.82), kind=kOutput, calls=%fused_computation.33 | convolution fusion | flops 1409286144 | bytes 9568256 | tf_op jit(solution)/shard_map/dot_general | solution.py:88
  297.8 92.3 %all-gather.15.cloned.1.call-done = bf16[2048,3584]{1,0:T(8,128)(2,1)} async-done(((bf16[256,3584]{1,0:T(8,128)(2,1)}), bf16[2048,3584]{1,0:T(8,128)(2,1)}) %all-gather.15.cloned.1.call-update) | async-done | bytes 14680080 | tf_op jit(solution)/shard_map/all_gather | solution.py:54
  390.1 9.4 %convolution_convert_fusion.1 = bf16[384,2048]{1,0:T(8,128)(2,1)S(1)} fusion(bf16[384,3584]{1,0:T(8,128)(2,1)S(1)} %copy-done, bf16[2048,3584]{1,0:T(8,128)(2,1)} %all-gather.15.cloned.1.call-done), kind=kOutput, calls=%fused_computation.9 | convolution fusion | flops 5637931008 | bytes 19005440 | tf_op jit(solution)/shard_map/dot_general | solution.py:16
  399.6 1.3 copy.41
  400.9 4.6 all-to-all-start.3
  405.5 3.1 reduce_sum.62
  408.6 95.9 %all-gather.13.cloned.1.call-done = bf16[3072,3584]{1,0:T(8,128)(2,1)} async-done(((bf16[384,3584]{1,0:T(8,128)(2,1)}), bf16[3072,3584]{1,0:T(8,128)(2,1)}) %all-gather.13.cloned.1.call-update) | async-done | bytes 22020112 | tf_op jit(solution)/shard_map/all_gather | solution.py:54
  504.5 14.0 %convolution_convert_fusion = bf16[384,3072]{1,0:T(8,128)(2,1)} fusion(bf16[384,3584]{1,0:T(8,128)(2,1)S(1)} %copy-done, bf16[3072,3584]{1,0:T(8,128)(2,1)} %all-gather.13.cloned.1.call-done), kind=kOutput, calls=%fused_computation.5 | convolution fusion | flops 8456896512 | bytes 27131904 | tf_op jit(solution)/shard_map/dot_general | solution.py:16
  518.6 3.2 copy.40
  521.8 4.7 all-to-all-start.2
  526.5 11.6 %fusion.9 = f32[384,3584]{1,0:T(8,128)} fusion(bf16[384,2048]{1,0:T(8,128)(2,1)S(1)} %bitcast.87, bf16[2048,3584]{1,0:T(8,128)(2,1)} %all-gather.15.cloned.1.call-done), kind=kOutput, calls=%fused_computation.34 | convolution fusion | flops 5637144576 | bytes 21757952 | tf_op jit(solution)/shard_map/dot_general | solution.py:98
  538.1 1.7 convert_reduce_fusion.1
  539.8 1.4 reshape.166
  541.2 4.2 all-gather.17.cloned.1.call-done
  545.4 2.4 slice.36
  547.8 2.3 slice.37
  550.1 18.7 %fusion.1 = bf16[384,3584]{1,0:T(8,128)(2,1)} fusion(f32[384,3584]{1,0:T(8,128)} %fusion.9, f32[384,3584]{1,0:T(8,128)} %fusion.8, bf16[384,3072]{1,0:T(8,128)(2,1)S(1)} %bitcast.85, bf16[3072,3584]{1,0:T(8,128)(2,1)} %all-gather.13.cloned.1.call-done), kind=kOutput, calls=%fused_computation.3 | convolution fusion | flops 8459845632 | bytes 38141952 | tf_op jit(solution)/shard_map/dot_general | solution.py:98
  568.8 12.2 %all-to-all-done.2 = bf16[4,384,768]{2,1,0:T(8,128)(2,1)} async-done(((bf16[4,384,768]{2,1,0:T(8,128)(2,1)}), bf16[4,384,768]{2,1,0:T(8,128)(2,1)}, u32[]{:S(2)}, u32[]{:S(2)}) %all-to-all-start.2) | async-done | bytes 2359328 | tf_op jit(solution)/shard_map/all_to_all | solution.py:93
  581.0 2.1 convert_reduce_fusion
  583.1 0.6 reshape.164
  583.8 2.0 pad_maximum_fusion.1
  585.9 1.2 copy-done.5
  587.1 1.6 fusion.2
  (42 shorter events, 2.1 us)
Async XLA Ops:
  7.2 131.6 %copy-start = (bf16[384,3584]{1,0:T(8,128)(2,1)S(1)}, bf16[384,3584]{1,0:T(8,128)(2,1)}, u32[]{:S(2)}) copy-start(bf16[384,3584]{1,0:T(8,128)(2,1)} %param.13) | copy-start | bytes 8257540
  17.4 33.8 %all-to-all-start = ((bf16[4,2,40960]{2,1,0:T(2,128)(2,1)}), bf16[4,2,40960]{2,1,0:T(2,128)(2,1)S(1)}, u32[]{:S(2)}, u32[]{:S(2)}) async-start(bf16[4,2,40960]{2,1,0:T(2,128)(2,1)} %reshape.171), calls=%async_computation | async-start | bytes 1310720 | tf_op jit(solution)/shard_map/all_to_all | solution.py:26
  51.3 47.2 %all-to-all-start.1 = ((bf16[4,2,114688]{2,1,0:T(2,128)(2,1)}), bf16[4,2,114688]{2,1,0:T(2,128)(2,1)}, u32[]{:S(2)}, u32[]{:S(2)}) async-start(bf16[4,2,114688]{2,1,0:T(2,128)(2,1)} %reshape.173), calls=%async_computation.1 | async-start | bytes 3670016 | tf_op jit(solution)/shard_map/all_to_all | solution.py:26
  56.4 70.4 %all-gather.7.cloned.1.call-start = ((), (), s32[]{:S(2)}) async-start(), calls=%async_computation.6 | async-start | bytes 1966080 | tf_op jit(solution)/shard_map/all_gather | solution.py:27
  66.1 72.6 %all-gather.9.cloned.1.call-start = ((), (), s32[]{:S(2)}) async-start(), calls=%async_computation.7 | async-start | bytes 5505024 | tf_op jit(solution)/shard_map/all_gather | solution.py:27
  123.5 3.1 copy-start.6
  126.6 60.1 %all-reduce.2.cloned.1.call-start = ((), (), s32[]{:S(2)}) async-start(), calls=%async_computation.8 | async-start | bytes 393216 | tf_op jit(solution)/shard_map/psum | solution.py:71
  146.6 4.6 copy-start.7
  150.3 113.9 %all-gather.11.cloned.1.call-start = ((), (), s32[]{:S(2)}) async-start(), calls=%async_computation.9 | async-start | bytes 4915200 | tf_op jit(solution)/shard_map/all_gather | solution.py:86
  150.9 131.6 %reduce-scatter.2.cloned.1.call-start = ((), (), s32[]{:S(2)}) async-start(), calls=%async_computation.12 | async-start | bytes 14942208 | tf_op jit(solution)/shard_map/reduce_scatter | solution.py:81
  209.6 180.5 %all-gather.15.cloned.1.call-start = ((), (), s32[]{:S(2)}) async-start(), calls=%async_computation.11 | async-start | bytes 16515072 | tf_op jit(solution)/shard_map/all_gather | solution.py:54
  212.6 291.9 %all-gather.13.cloned.1.call-start = ((), (), s32[]{:S(2)}) async-start(), calls=%async_computation.10 | async-start | bytes 24772608 | tf_op jit(solution)/shard_map/all_gather | solution.py:54
  286.6 114.2 %all-to-all-start.4 = ((bf16[4,64,4864]{2,1,0:T(8,128)(2,1)}), bf16[4,64,4864]{2,1,0:T(8,128)(2,1)}, u32[]{:S(2)}, u32[]{:S(2)}) async-start(bf16[4,64,4864]{2,1,0:T(8,128)(2,1)} %bitcast.71), calls=%async_computation.5 | async-start | bytes 4980736 | tf_op jit(solution)/shard_map/all_to_all | solution.py:32
  400.9 120.9 %all-to-all-start.3 = ((bf16[4,384,512]{2,1,0:T(8,128)(2,1)}), bf16[4,384,512]{2,1,0:T(8,128)(2,1)}, u32[]{:S(2)}, u32[]{:S(2)}) async-start(bf16[4,384,512]{2,1,0:T(8,128)(2,1)} %bitcast.77), calls=%async_computation.3 | async-start | bytes 3145728 | tf_op jit(solution)/shard_map/all_to_all | solution.py:93
  405.5 139.9 %all-gather.17.cloned.1.call-start = ((), (), s32[]{:S(2)}) async-start(), calls=%async_computation.13 | async-start | bytes 3112960 | tf_op jit(solution)/shard_map/all_gather | solution.py:36
  521.8 4.7 copy-start.4
  521.8 59.2 %all-to-all-start.2 = ((bf16[4,384,768]{2,1,0:T(8,128)(2,1)}), bf16[4,384,768]{2,1,0:T(8,128)(2,1)}, u32[]{:S(2)}, u32[]{:S(2)}) async-start(bf16[4,384,768]{2,1,0:T(8,128)(2,1)} %bitcast.62), calls=%async_computation.2 | async-start | bytes 4718592 | tf_op jit(solution)/shard_map/all_to_all | solution.py:93
  545.4 2.4 copy-start.2
  547.8 2.3 copy-start.3
  585.8 1.3 copy-start.5
  585.8 2.9 copy-start.1
Sparse Core Ops, SparseCore 0:
  66.2 10.8 all-gather.6
  126.7 11.9 all-gather.8
  150.5 36.1 all-reduce.1
  188.1 76.0 all-gather.10
  266.4 16.1 reduce-scatter.1
  284.3 105.8 all-gather.14
  392.6 111.8 all-gather.12
  506.9 38.4 all-gather.16
